TPU v7x, 32 devices: a whole 2x2x4 slice. The times are simulated.
32 devices in a mesh: mat: 4 (over x, core), frac: 8 (over z, y).
Axes of the slice: x: 2, y: 2, z: 4, core: 2. Of those that a mesh axis runs over, the one named last changes fastest.
Arguments:
- pressure_start: float32 [64, 512, 256], P('mat', 'frac'), may hold values from -6 to 6
- face_trans: float32 [3, 64, 512, 256], P(None, 'mat', 'frac'), may hold values from 0.2 to 2
- cell_coef: float32 [64, 512, 256], P('mat', 'frac'), may hold values from 0.05 to 0.5
- matrix_source: float32 [64, 512, 256], P('mat', 'frac'), may hold values from -6 to 6
- mortar_owner: int32 [16384, 1], P(('mat', 'frac')), may hold values from 0 to 31; in each aligned block of 512 rows (0 to 511, 512 to 1023, ...) at most 32 rows name the same one
- mortar_cell: int32 [16384], P(('mat', 'frac')), may hold values from 0 to 262143
- mortar_frac: int32 [16384], P(('mat', 'frac')), may hold values from 0 to 8191
- mortar_kappa: float32 [16384], P(('mat', 'frac')), may hold values from 0.5 to 2
- tiles: float32 [64, 4, 128, 128], P('frac'), may hold values from -0.25 to 0.25
- tile_cols: int32 [64, 4], P('frac'), may hold values from 0 to 63
- frac_diag: float32 [8192], P('frac'), may hold values from 4 to 8
- frac_source: float32 [8192], P('frac'), may hold values from -6 to 6
- fracture_start: float32 [8192], P('frac'), may hold values from -6 to 6
Outputs:
- pressure: float32 [64, 512, 256], P('mat', 'frac')
- fracture: float32 [8192], P('frac')
- flux: float32 [16384], P(('mat', 'frac'))
Inputs may be any that keep to these rules, and one draw needn't show every extreme that they name: `mortar_owner`: among the 512 mortar cells of one device, at most 32 name the same owner, and in some devices some owner is named exactly 32 times.
All inputs are finite; a program needn't handle non-finite values.
Results may differ from a plain program's by a relative error of at most 0.00015.
Values sent between devices are 32-bit elements; how exact they have to be, the bound alone decides.
A program may use at most 128 MiB of HBM per device.

v0:
```python
import jax
import jax.numpy as jnp
from jax import lax
from jax.sharding import PartitionSpec as P

SWEEPS = 2
CG_ITERS = 3
OUTER = 2
relax_weight = 0.8


def shifted(value, axis, steps):
    count = lax.axis_size(axis)
    leading, last = (max(0, -steps), min(count, count - steps))
    return lax.ppermute(value, axis, [(source, source + steps) for source in range(leading, last)])


def with_halo(block, sides, width):
    for axis, dim in sides:
        count = lax.axis_size(axis)
        forward = [(i, i + 1) for i in range(count - 1)]
        backward = [(target, source) for source, target in forward]
        low = lax.ppermute(
            lax.slice_in_dim(block, block.shape[dim] - width, None, axis=dim), axis, forward
        )
        high = lax.ppermute(lax.slice_in_dim(block, 0, width, axis=dim), axis, backward)
        block = jnp.concatenate([low, block, high], axis=dim)
    return block


def shift_next(values, along):
    padding = [(0, 0)] * values.ndim
    padding[along] = (0, 1)
    return lax.slice_in_dim(jnp.pad(values, padding), 1, values.shape[along] + 1, axis=along)


def shift_prev(values, along):
    padding = [(0, 0)] * values.ndim
    padding[along] = (1, 0)
    return lax.slice_in_dim(jnp.pad(values, padding), 0, values.shape[along], axis=along)


def relax(padded, coef_part, source_part, inside):
    centre = padded[1:-1, 1:-1]
    tx_here = coef_part[0, 1:-1, 1:-1]
    tx_low = coef_part[0, :-2, 1:-1]
    ty_here = coef_part[1, 1:-1, 1:-1]
    ty_low = coef_part[1, 1:-1, :-2]
    tz_here = coef_part[2, 1:-1, 1:-1]
    tz_low = shift_prev(tz_here, 2)
    cell_part = coef_part[3, 1:-1, 1:-1]
    base_part = coef_part[4, 1:-1, 1:-1]
    diagonal = cell_part + tx_here + tx_low + ty_here + ty_low + tz_here + tz_low
    diagonal = jnp.where(inside, diagonal, 1.0)
    applied = (
        diagonal * centre
        - tx_here * padded[2:, 1:-1]
        - tx_low * padded[:-2, 1:-1]
        - ty_here * padded[1:-1, 2:]
        - ty_low * padded[1:-1, :-2]
        - tz_here * shift_next(centre, 2)
        - tz_low * shift_prev(centre, 2)
    )
    updated = centre + relax_weight * (base_part + source_part - applied) / diagonal
    return jnp.where(inside, updated, 0.0)


def body(
    pressure_start,
    face_trans,
    cell_coef,
    matrix_source,
    mortar_owner,
    mortar_cell,
    mortar_frac,
    mortar_kappa,
    tiles,
    tile_cols,
    frac_diag,
    frac_source,
    fracture_start,
):
    width_x, width_y, depth_z = pressure_start.shape
    cells = width_x * width_y * depth_z
    mat_count = lax.axis_size("mat")
    frac_count = lax.axis_size("frac")
    devices = mat_count * frac_count
    row_mat = lax.axis_index("mat")
    row_frac = lax.axis_index("frac")
    size_b = tiles.shape[2]
    coefs = jnp.concatenate([face_trans, cell_coef[None], matrix_source[None]], 0)
    lower_x = shifted(face_trans[0, -1], "mat", 1)
    lower_y = shifted(face_trans[1, :, -1], "frac", 1)
    coef_ext = jnp.pad(coefs, ((0, 0), (1, 1), (1, 1), (0, 0)))
    coef_ext = coef_ext.at[0, 0, 1:-1].set(lower_x)
    coef_ext = coef_ext.at[1, 1:-1, 0].set(lower_y)
    owner = mortar_owner[:, 0]
    mortar_count = owner.shape[0]
    capacity = max(2, 2 * mortar_count // devices)
    hits = (owner[:, None] == jnp.arange(devices, dtype=jnp.int32)[None, :]).astype(jnp.int32)
    ranks = jnp.cumsum(hits, axis=0)
    slot = jnp.sum(ranks * hits, axis=1) - 1
    place = owner * capacity + slot
    index_slots = (
        jnp.full((devices * capacity,), cells, jnp.int32)
        .at[place]
        .set(mortar_cell)
        .reshape(devices, capacity)
    )
    asked = lax.all_to_all(index_slots, ("mat", "frac"), split_axis=0, concat_axis=0, tiled=True)
    asked_safe = jnp.minimum(asked, cells - 1)

    def fracture_apply(vector):
        whole = lax.all_gather(vector, "frac", axis=0, tiled=True)
        blocks = whole.reshape(-1, size_b)
        forward = jnp.einsum(
            "rtij,rtj->ri", tiles, blocks[tile_cols], precision=lax.Precision.HIGHEST
        )
        backward = jnp.einsum(
            "rtij,ri->rtj", tiles, vector.reshape(-1, size_b), precision=lax.Precision.HIGHEST
        )
        spread = jnp.zeros_like(blocks).at[tile_cols.reshape(-1)].add(backward.reshape(-1, size_b))
        returned = lax.psum_scatter(spread, "frac", scatter_dimension=0, tiled=True)
        return frac_diag * vector + 0.5 * (forward + returned).reshape(-1)

    def two_products(residual, image):
        return lax.psum((jnp.sum(residual * residual), jnp.sum(residual * image)), "frac")

    def solve_fracture(fracture, target):
        residual = target - fracture_apply(fracture)
        image = fracture_apply(residual)
        norm_now, product = two_products(residual, image)
        alpha = norm_now / product
        direction, along_image = (residual, image)
        for step in range(CG_ITERS):
            fracture = fracture + alpha * direction
            residual = residual - alpha * along_image
            if step + 1 < CG_ITERS:
                image = fracture_apply(residual)
                norm_next, product = two_products(residual, image)
                ratio = norm_next / norm_now
                alpha = norm_next / (product - ratio * norm_next / alpha)
                direction = residual + ratio * direction
                along_image = image + ratio * along_image
                norm_now = norm_next
        return fracture

    pressure = pressure_start
    fracture = fracture_start
    flux = jnp.zeros(mortar_kappa.shape, jnp.float32)
    for outer_no in range(OUTER):
        local_values = pressure.reshape(-1)[asked_safe]
        returned = lax.all_to_all(
            local_values, ("mat", "frac"), split_axis=0, concat_axis=0, tiled=True
        )
        trace = returned.reshape(-1)[place]
        fracture_whole = lax.all_gather(fracture, "frac", axis=0, tiled=True)
        flux = mortar_kappa * (trace - fracture_whole[mortar_frac])
        landed = jax.ops.segment_sum(flux, mortar_frac, num_segments=fracture_whole.shape[0])
        summed = lax.psum(landed, ("mat", "frac"))
        load = lax.dynamic_slice_in_dim(summed, row_frac * fracture.shape[0], fracture.shape[0])
        fracture = solve_fracture(fracture, frac_source + load)
        flux_slots = (
            jnp.zeros((devices * capacity,), jnp.float32)
            .at[place]
            .set(flux)
            .reshape(devices, capacity)
        )
        arrived = lax.all_to_all(
            flux_slots, ("mat", "frac"), split_axis=0, concat_axis=0, tiled=True
        )
        source = jax.ops.segment_sum(
            arrived.reshape(-1), asked_safe.reshape(-1), num_segments=cells
        ).reshape(pressure.shape)
        for sweep_no in range(SWEEPS):
            padded = with_halo(pressure, (("mat", 0), ("frac", 1)), 1)
            global_x = row_mat * width_x - 0 + jnp.arange(width_x)
            global_y = row_frac * width_y - 0 + jnp.arange(width_y)
            keep_x = (global_x >= 0) & (global_x < width_x * mat_count)
            keep_y = (global_y >= 0) & (global_y < width_y * frac_count)
            pressure = relax(
                padded, coef_ext, source, (keep_x[:, None] & keep_y[None, :])[:, :, None]
            )
    return (pressure, fracture, flux)


def solution(mesh):
    in_specs = (
        P("mat", "frac", None),
        P(None, "mat", "frac", None),
        P("mat", "frac", None),
        P("mat", "frac", None),
        P(("mat", "frac"), None),
        P(("mat", "frac")),
        P(("mat", "frac")),
        P(("mat", "frac")),
        P("frac", None, None, None),
        P("frac", None),
        P("frac"),
        P("frac"),
        P("frac"),
    )
    out_specs = (P("mat", "frac", None), P("frac"), P(("mat", "frac")))
    return jax.shard_map(body, mesh=mesh, in_specs=in_specs, out_specs=out_specs, check_vma=False)
```

profile of v0, /device:TPU:0, one launch (start us, length us, event | category | flops | bytes accessed | tf_op | source)
XLA Modules:
  0.0 977.3 jit_solution(13991142482101642097)
XLA Ops:
  5.7 4.2 collective-permute-start.1
  11.5 3.4 collective-permute-start.3
  23.1 5.9 all-to-all-start
  30.5 31.1 %all_gather.26 = f32[8192]{0:T(1024)S(1)} all-gather(f32[1024]{0:T(1024)} %param.29), channel_id=1, replica_groups=mesh['mat'=4,'frac'=8] {'frac'}, dimensions={0}, use_global_device_ids=true | all-gather | bytes 36864 | tf_op jit(solution)/shard_map/all_gather | solution.py:157
  66.3 3.3 select_maximum_fusion
  71.0 6.1 gather_fusion
  77.9 5.5 all-to-all-start.1
  83.4 37.4 %all-reduce.10 = f32[64,128]{1,0:T(8,128)S(1)} all-reduce(f32[64,128]{1,0:T(8,128)S(1)} %scatter_custom_fusion.4), channel_id=2, replica_groups=mesh['mat'=4,'frac'=8] {'frac'}, use_global_device_ids=true, to_apply=%region_9.10.clone | all-reduce | flops 8192 | bytes 65536
  120.8 3.1 gather_fusion.2
  131.4 3.4 scatter_custom_fusion.3
  138.0 40.6 %psum.98 = f32[8192]{0:T(1024)S(1)} all-reduce(f32[8192]{0:T(1024)S(1)} %scatter_custom_fusion.3), channel_id=1, replica_groups=mesh['mat'=4,'frac'=8] {'mat','frac'}, use_global_device_ids=true, to_apply=%region_7.8 | all-reduce | flops 8192 | bytes 65536 | tf_op jit(solution)/shard_map/psum | solution.py:160
  178.7 30.8 %all_gather.27 = f32[8192]{0:T(1024)S(1)} all-gather(f32[1024]{0:T(1024)S(1)} %fusion.134), channel_id=1, replica_groups=mesh['mat'=4,'frac'=8] {'frac'}, dimensions={0}, use_global_device_ids=true | all-gather | bytes 36864 | tf_op jit(solution)/shard_map/all_gather | solution.py:114
  213.7 36.8 %all-reduce.11 = f32[64,128]{1,0:T(8,128)S(1)} all-reduce(f32[64,128]{1,0:T(8,128)S(1)} %scatter_custom_fusion.5), channel_id=3, replica_groups=mesh['mat'=4,'frac'=8] {'frac'}, use_global_device_ids=true, to_apply=%region_13.14.clone | all-reduce | flops 8192 | bytes 65536
  251.2 17.8 %all-reduce.23 = (f32[]{:T(128)}, f32[]{:T(128)}) all-reduce(f32[]{:T(128)} %get-tuple-element.38, f32[]{:T(128)} %get-tuple-element.37), channel_id=1, replica_groups=mesh['mat'=4,'frac'=8] {'frac'}, use_global_device_ids=true, to_apply=%region_11.12 | all-reduce | flops 2 | bytes 16 | tf_op jit(solution)/shard_map/psum | solution.py:127
  270.3 30.6 %all_gather.28 = f32[8192]{0:T(1024)S(1)} all-gather(f32[1024]{0:T(1024)S(1)} %multiply_subtract_fusion.3), channel_id=1, replica_groups=mesh['mat'=4,'frac'=8] {'frac'}, dimensions={0}, use_global_device_ids=true | all-gather | bytes 36864 | tf_op jit(solution)/shard_map/all_gather | solution.py:114
  305.1 34.9 %all-reduce.12 = f32[64,128]{1,0:T(8,128)S(1)} all-reduce(f32[64,128]{1,0:T(8,128)S(1)} %scatter_custom_fusion.6), channel_id=4, replica_groups=mesh['mat'=4,'frac'=8] {'frac'}, use_global_device_ids=true, to_apply=%region_19.20.clone | all-reduce | flops 8192 | bytes 65536
  340.7 17.8 %all-reduce.22 = (f32[]{:T(128)}, f32[]{:T(128)}) all-reduce(f32[]{:T(128)} %get-tuple-element.36, f32[]{:T(128)} %get-tuple-element.35), channel_id=1, replica_groups=mesh['mat'=4,'frac'=8] {'frac'}, use_global_device_ids=true, to_apply=%region_17.18 | all-reduce | flops 2 | bytes 16 | tf_op jit(solution)/shard_map/psum | solution.py:127
  362.9 30.6 %all_gather.29 = f32[8192]{0:T(1024)S(1)} all-gather(f32[1024]{0:T(1024)S(1)} %multiply_subtract_fusion.2), channel_id=1, replica_groups=mesh['mat'=4,'frac'=8] {'frac'}, dimensions={0}, use_global_device_ids=true | all-gather | bytes 36864 | tf_op jit(solution)/shard_map/all_gather | solution.py:114
  397.8 34.9 %all-reduce.13 = f32[64,128]{1,0:T(8,128)S(1)} all-reduce(f32[64,128]{1,0:T(8,128)S(1)} %scatter_custom_fusion.7), channel_id=5, replica_groups=mesh['mat'=4,'frac'=8] {'frac'}, use_global_device_ids=true, to_apply=%region_25.26.clone | all-reduce | flops 8192 | bytes 65536
  433.3 17.8 %all-reduce.21 = (f32[]{:T(128)}, f32[]{:T(128)}) all-reduce(f32[]{:T(128)} %get-tuple-element.34, f32[]{:T(128)} %get-tuple-element.33), channel_id=1, replica_groups=mesh['mat'=4,'frac'=8] {'frac'}, use_global_device_ids=true, to_apply=%region_23.24 | all-reduce | flops 2 | bytes 16 | tf_op jit(solution)/shard_map/psum | solution.py:127
  454.9 30.6 %all_gather.30 = f32[8192]{0:T(1024)S(1)} all-gather(f32[1024]{0:T(1024)S(1)} %multiply_add_fusion.1), channel_id=1, replica_groups=mesh['mat'=4,'frac'=8] {'frac'}, dimensions={0}, use_global_device_ids=true | all-gather | bytes 36864 | tf_op jit(solution)/shard_map/all_gather | solution.py:157
  486.8 7.2 scatter_custom_fusion.2
  505.6 7.6 broadcast_select_fusion.1
  514.6 3.0 collective-permute-start.7
  519.5 4.5 collective-permute-start.9
  526.4 3.1 gather_fusion.9
  530.4 37.6 %all-reduce.14 = f32[64,128]{1,0:T(8,128)S(1)} all-reduce(f32[64,128]{1,0:T(8,128)S(1)} %scatter_custom_fusion.11), channel_id=6, replica_groups=mesh['mat'=4,'frac'=8] {'frac'}, use_global_device_ids=true, to_apply=%region_33.34.clone | all-reduce | flops 8192 | bytes 65536
  568.1 8.4 fusion.75
  578.0 6.2 gather_fusion.3
  589.6 3.0 collective-permute-start.11
  600.2 3.4 scatter_custom_fusion.10
  604.3 4.0 all-to-all-start.4
  608.3 41.0 %psum.105 = f32[8192]{0:T(1024)S(1)} all-reduce(f32[8192]{0:T(1024)S(1)} %scatter_custom_fusion.10), channel_id=1, replica_groups=mesh['mat'=4,'frac'=8] {'mat','frac'}, use_global_device_ids=true, to_apply=%region_31.32 | all-reduce | flops 8192 | bytes 65536 | tf_op jit(solution)/shard_map/psum | solution.py:160
  649.3 30.6 %all_gather.31 = f32[8192]{0:T(1024)S(1)} all-gather(f32[1024]{0:T(1024)S(1)} %fusion.119), channel_id=1, replica_groups=mesh['mat'=4,'frac'=8] {'frac'}, dimensions={0}, use_global_device_ids=true | all-gather | bytes 36864 | tf_op jit(solution)/shard_map/all_gather | solution.py:114
  684.3 36.9 %all-reduce.15 = f32[64,128]{1,0:T(8,128)S(1)} all-reduce(f32[64,128]{1,0:T(8,128)S(1)} %scatter_custom_fusion.12), channel_id=7, replica_groups=mesh['mat'=4,'frac'=8] {'frac'}, use_global_device_ids=true, to_apply=%region_37.38.clone | all-reduce | flops 8192 | bytes 65536
  721.9 17.8 %all-reduce.20 = (f32[]{:T(128)}, f32[]{:T(128)}) all-reduce(f32[]{:T(128)} %get-tuple-element.32, f32[]{:T(128)} %get-tuple-element.31), channel_id=1, replica_groups=mesh['mat'=4,'frac'=8] {'frac'}, use_global_device_ids=true, to_apply=%region_35.36 | all-reduce | flops 2 | bytes 16 | tf_op jit(solution)/shard_map/psum | solution.py:127
  741.0 30.6 %all_gather.32 = f32[8192]{0:T(1024)S(1)} all-gather(f32[1024]{0:T(1024)S(1)} %multiply_subtract_fusion.1), channel_id=1, replica_groups=mesh['mat'=4,'frac'=8] {'frac'}, dimensions={0}, use_global_device_ids=true | all-gather | bytes 36864 | tf_op jit(solution)/shard_map/all_gather | solution.py:114
  776.0 34.9 %all-reduce.16 = f32[64,128]{1,0:T(8,128)S(1)} all-reduce(f32[64,128]{1,0:T(8,128)S(1)} %scatter_custom_fusion.13), channel_id=8, replica_groups=mesh['mat'=4,'frac'=8] {'frac'}, use_global_device_ids=true, to_apply=%region_43.44.clone | all-reduce | flops 8192 | bytes 65536
  811.5 17.8 %all-reduce.19 = (f32[]{:T(128)}, f32[]{:T(128)}) all-reduce(f32[]{:T(128)} %get-tuple-element.30, f32[]{:T(128)} %get-tuple-element.29), channel_id=1, replica_groups=mesh['mat'=4,'frac'=8] {'frac'}, use_global_device_ids=true, to_apply=%region_41.42 | all-reduce | flops 2 | bytes 16 | tf_op jit(solution)/shard_map/psum | solution.py:127
  834.0 30.6 %all_gather.33 = f32[8192]{0:T(1024)S(1)} all-gather(f32[1024]{0:T(1024)S(1)} %multiply_subtract_fusion), channel_id=1, replica_groups=mesh['mat'=4,'frac'=8] {'frac'}, dimensions={0}, use_global_device_ids=true | all-gather | bytes 36864 | tf_op jit(solution)/shard_map/all_gather | solution.py:114
  871.8 38.1 %all-reduce.17 = f32[64,128]{1,0:T(8,128)S(1)} all-reduce(f32[64,128]{1,0:T(8,128)S(1)} %scatter_custom_fusion.14), channel_id=9, replica_groups=mesh['mat'=4,'frac'=8] {'frac'}, use_global_device_ids=true, to_apply=%region_49.50.clone | all-reduce | flops 8192 | bytes 65536
  910.7 7.6 scatter_custom_fusion.9
  920.7 8.4 broadcast_select_fusion
  931.6 3.0 collective-permute-start.15
  935.2 17.8 %all-reduce.18 = (f32[]{:T(128)}, f32[]{:T(128)}) all-reduce(f32[]{:T(128)} %get-tuple-element.28, f32[]{:T(128)} %get-tuple-element.27), channel_id=1, replica_groups=mesh['mat'=4,'frac'=8] {'frac'}, use_global_device_ids=true, to_apply=%region_47.48 | all-reduce | flops 2 | bytes 16 | tf_op jit(solution)/shard_map/psum | solution.py:127
  958.0 3.9 collective-permute-start.17
  963.9 3.7 collective-permute-done.16
  967.6 9.4 fusion.74
  (205 shorter events, 108.2 us)
Async XLA Ops:
  0.6 62.5 %copy-start = (f32[8,4,128,128]{3,2,1,0:T(8,128)S(1)}, f32[8,4,128,128]{3,2,1,0:T(8,128)}, u32[]{:S(2)}) copy-start(f32[8,4,128,128]{3,2,1,0:T(8,128)} %param.25) | copy-start | bytes 6291460
  0.6 64.4 %copy-start.15 = (f32[1024]{0:T(1024)S(1)}, f32[1024]{0:T(1024)}, u32[]{:S(2)}) copy-start(f32[1024]{0:T(1024)} %param.29) | copy-start | bytes 12292
  2.3 498.6 %collective-permute-start = (f32[64,256]{1,0:T(8,128)}, f32[64,256]{1,0:T(8,128)S(1)}, u32[]{:S(2)}, u32[]{:S(2)}) collective-permute-start(f32[64,256]{1,0:T(8,128)} %slice_bitcast_fusion.7), channel_id=1, source_target_pairs={{0,8},{8,16},{16,24},{1,9},{9,17},{17,25},{2,10},{10,18},{18,26},{... | collective-permute-start | bytes 196616 | tf_op jit(solution)/shard_map/ppermute | solution.py:15
  4.7 61.6 %copy-start.13 = (f32[16,64,256]{2,1,0:T(8,128)S(1)}, f32[16,64,256]{2,1,0:T(8,128)}, u32[]{:S(2)}) copy-start(f32[16,64,256]{2,1,0:T(8,128)} %param.19) | copy-start | bytes 3145732
  5.7 480.3 %collective-permute-start.1 = (f32[16,256]{1,0:T(8,128)S(1)}, f32[16,256]{1,0:T(8,128)S(1)}, u32[]{:S(2)}, u32[]{:S(2)}) collective-permute-start(f32[16,256]{1,0:T(8,128)S(1)} %bitcast.415), channel_id=1, source_target_pairs={{0,1},{1,2},{2,3},{3,4},{4,5},{5,6},{6,7},{8,9},{9,10},{10,11},{11... | collective-permute-start | bytes 49160 | tf_op jit(solution)/shard_map/ppermute | solution.py:15
  11.5 485.1 %collective-permute-start.3 = (f32[1,64,256]{2,1,0:T(8,128)}, f32[1,64,256]{2,1,0:T(8,128)S(1)}, u32[]{:S(2)}, u32[]{:S(2)}) collective-permute-start(f32[1,64,256]{2,1,0:T(8,128)} %get-tuple-element.72), channel_id=1, source_target_pairs={{0,8},{8,16},{16,24},{1,9},{9,17},{17,25},{2,10},{10,18},{18,26},{... | collective-permute-start | bytes 196616 | tf_op jit(solution)/shard_map/ppermute | solution.py:23
  14.9 481.9 %collective-permute-start.2 = (f32[1,64,256]{2,1,0:T(8,128)}, f32[1,64,256]{2,1,0:T(8,128)S(1)}, u32[]{:S(2)}, u32[]{:S(2)}) collective-permute-start(f32[1,64,256]{2,1,0:T(8,128)} %get-tuple-element.71), channel_id=1, source_target_pairs={{8,0},{16,8},{24,16},{9,1},{17,9},{25,17},{10,2},{18,10},{26,18},{... | collective-permute-start | bytes 196616 | tf_op jit(solution)/shard_map/ppermute | solution.py:26
  19.8 109.1 %copy-start.20 = (s32[512,1]{0,1:T(1,128)}, s32[512,1]{0,1:T(1,128)S(1)}, u32[]{:S(2)}) copy-start(s32[512,1]{0,1:T(1,128)S(1)} %compare_select_fusion.1) | copy-start | bytes 6148
  23.1 47.8 %all-to-all-start = ((s32[32,1,32]{2,1,0:T(1,128)}), s32[32,1,32]{2,1,0:T(1,128)S(1)}, u32[]{:S(2)}, u32[]{:S(2)}) async-start(s32[32,1,32]{2,1,0:T(1,128)} %all_to_all.30), calls=%async_computation | async-start | bytes 32768 | tf_op jit(solution)/shard_map/all_to_all | solution.py:110
  29.0 97.5 %copy-start.18 = (s32[1024]{0:T(1024)}, s32[1024]{0:T(1024)S(1)}, u32[]{:S(2)}) copy-start(s32[1024]{0:T(1024)S(1)} %pad_clamp_fusion.2) | copy-start | bytes 12292
  62.6 334.5 %copy-start.25 = (s32[32]{0:T(128)}, s32[32]{0:T(128)S(1)}, u32[]{:S(2)}) copy-start(s32[32]{0:T(128)S(1)} %fusion.141) | copy-start | bytes 388
  63.1 3.1 copy-start.9
  63.2 3.1 copy-start.12
  66.3 3.3 copy-start.7
  77.2 46.8 %copy-start.26 = (u32[32]{0:T(128)S(1)}, u32[32]{0:T(128)}, u32[]{:S(2)}) copy-start(u32[32]{0:T(128)} %constant.147) | copy-start | bytes 388
  77.9 47.4 %all-to-all-start.1 = ((f32[32,1,32]{2,1,0:T(1,128)}), f32[32,1,32]{2,1,0:T(1,128)S(1)}, u32[]{:S(2)}, u32[]{:S(2)}) async-start(f32[32,1,32]{2,1,0:T(1,128)} %all_to_all.32), calls=%async_computation.1 | async-start | bytes 32768 | tf_op jit(solution)/shard_map/all_to_all | solution.py:153
  120.8 8.1 copy-start.21
  120.8 57.9 %copy-start.14 = (f32[1024]{0:T(1024)S(1)}, f32[1024]{0:T(1024)}, u32[]{:S(2)}) copy-start(f32[1024]{0:T(1024)} %param.27) | copy-start | bytes 12292
  120.8 57.9 %copy-start.16 = (f32[1024]{0:T(1024)S(1)}, f32[1024]{0:T(1024)}, u32[]{:S(2)}) copy-start(f32[1024]{0:T(1024)} %param.28) | copy-start | bytes 12292
  125.3 361.5 %copy-start.23 = (s32[1024]{0:T(1024)}, s32[1024]{0:T(1024)S(1)}, u32[]{:S(2)}) copy-start(s32[1024]{0:T(1024)S(1)} %reshape.528) | copy-start | bytes 12292
  135.5 350.6 %all-to-all-start.2 = ((f32[32,1,32]{2,1,0:T(1,128)}), f32[32,1,32]{2,1,0:T(1,128)S(1)}, u32[]{:S(2)}, u32[]{:S(2)}) async-start(f32[32,1,32]{2,1,0:T(1,128)} %all_to_all.34), calls=%async_computation.2 | async-start | bytes 32768 | tf_op jit(solution)/shard_map/all_to_all | solution.py:169
  397.0 99.6 %copy-start.8 = (f32[16,64,256]{2,1,0:T(8,128)S(1)}, f32[16,64,256]{2,1,0:T(8,128)}, u32[]{:S(2)}) copy-start(f32[16,64,256]{2,1,0:T(8,128)} %param.17) | copy-start | bytes 3145732
  497.8 7.7 collective-permute-start.5
  499.5 5.9 collective-permute-start.4
  504.0 1.6 copy-start.11
  505.4 62.6 %copy-start.1 = (f32[16,64,256]{2,1,0:T(8,128)}, f32[16,64,256]{2,1,0:T(8,128)S(1)}, u32[]{:S(2)}) copy-start(f32[16,64,256]{2,1,0:T(8,128)S(1)} %slice_bitcast_fusion) | copy-start | bytes 3145732
  513.2 6.2 copy-start.6
  513.3 6.2 collective-permute-start.6
  514.6 4.9 collective-permute-start.7
  519.5 48.6 %collective-permute-start.9 = (f32[18,1,256]{2,1,0:T(1,128)S(1)}, f32[18,1,256]{2,1,0:T(1,128)S(1)}, u32[]{:S(2)}, u32[]{:S(2)}) collective-permute-start(f32[18,1,256]{2,1,0:T(1,128)S(1)} %get-tuple-element.62), channel_id=1, source_target_pairs={{0,1},{1,2},{2,3},{3,4},{4,5},{5,6},{6,7},{8,9},{9,10},{10,11},{11... | collective-permute-start | bytes 55304 | tf_op jit(solution)/shard_map/ppermute | solution.py:23
  524.0 44.0 %collective-permute-start.8 = (f32[18,1,256]{2,1,0:T(1,128)S(1)}, f32[18,1,256]{2,1,0:T(1,128)S(1)}, u32[]{:S(2)}, u32[]{:S(2)}) collective-permute-start(f32[18,1,256]{2,1,0:T(1,128)S(1)} %get-tuple-element.61), channel_id=1, source_target_pairs={{1,0},{2,1},{3,2},{4,3},{5,4},{6,5},{7,6},{9,8},{10,9},{11,10},{12... | collective-permute-start | bytes 55304 | tf_op jit(solution)/shard_map/ppermute | solution.py:26
  578.0 17.3 %copy-start.19 = (s32[1024]{0:T(1024)S(1)}, s32[1024]{0:T(1024)}, u32[]{:S(2)}) copy-start(s32[1024]{0:T(1024)} %copy-done.18) | copy-start | bytes 12292
  584.1 13.4 %copy-start.22 = (f32[512]{0:T(512)S(1)}, f32[512]{0:T(512)}, u32[]{:S(2)}) copy-start(f32[512]{0:T(512)} %param.24) | copy-start | bytes 6148
  584.1 65.2 %copy-start.17 = (f32[1024]{0:T(1024)S(1)}, f32[1024]{0:T(1024)}, u32[]{:S(2)}) copy-start(f32[1024]{0:T(1024)} %param.28) | copy-start | bytes 12292
  584.8 9.7 all-to-all-start.3
  588.3 278.8 %collective-permute-start.10 = (f32[1,64,256]{2,1,0:T(8,128)S(1)}, f32[1,64,256]{2,1,0:T(8,128)S(1)}, u32[]{:S(2)}, u32[]{:S(2)}) collective-permute-start(f32[1,64,256]{2,1,0:T(8,128)S(1)} %get-tuple-element.68), channel_id=1, source_target_pairs={{8,0},{16,8},{24,16},{9,1},{17,9},{25,17},{10,2},{18,10},{26,18},{... | collective-permute-start | bytes 196616 | tf_op jit(solution)/shard_map/ppermute | solution.py:26
  589.6 277.5 %collective-permute-start.11 = (f32[1,64,256]{2,1,0:T(8,128)S(1)}, f32[1,64,256]{2,1,0:T(8,128)S(1)}, u32[]{:S(2)}, u32[]{:S(2)}) collective-permute-start(f32[1,64,256]{2,1,0:T(8,128)S(1)} %get-tuple-element.67), channel_id=1, source_target_pairs={{0,8},{8,16},{16,24},{1,9},{9,17},{17,25},{2,10},{10,18},{18,26},{... | collective-permute-start | bytes 196616 | tf_op jit(solution)/shard_map/ppermute | solution.py:23
  597.6 85.9 %copy-start.24 = (f32[512]{0:T(512)}, f32[512]{0:T(512)S(1)}, u32[]{:S(2)}) copy-start(f32[512]{0:T(512)S(1)} %subtract_multiply_fusion) | copy-start | bytes 6148
  604.3 305.6 %all-to-all-start.4 = ((f32[32,1,32]{2,1,0:T(1,128)}), f32[32,1,32]{2,1,0:T(1,128)S(1)}, u32[]{:S(2)}, u32[]{:S(2)}) async-start(f32[32,1,32]{2,1,0:T(1,128)} %all_to_all.38), calls=%async_computation.4 | async-start | bytes 32768 | tf_op jit(solution)/shard_map/all_to_all | solution.py:169
  774.0 93.1 %copy-start.4 = (f32[16,64,256]{2,1,0:T(8,128)S(1)}, f32[16,64,256]{2,1,0:T(8,128)}, u32[]{:S(2)}) copy-start(f32[16,64,256]{2,1,0:T(8,128)} %copy-done.3) | copy-start | bytes 3145732
  867.1 53.6 %collective-permute-start.13 = (f32[18,1,256]{2,1,0:T(1,128)S(1)}, f32[18,1,256]{2,1,0:T(1,128)S(1)}, u32[]{:S(2)}, u32[]{:S(2)}) collective-permute-start(f32[18,1,256]{2,1,0:T(1,128)S(1)} %get-tuple-element.60), channel_id=1, source_target_pairs={{0,1},{1,2},{2,3},{3,4},{4,5},{5,6},{6,7},{8,9},{9,10},{10,11},{11... | collective-permute-start | bytes 55304 | tf_op jit(solution)/shard_map/ppermute | solution.py:23
  868.4 52.3 %collective-permute-start.12 = (f32[18,1,256]{2,1,0:T(1,128)S(1)}, f32[18,1,256]{2,1,0:T(1,128)S(1)}, u32[]{:S(2)}, u32[]{:S(2)}) collective-permute-start(f32[18,1,256]{2,1,0:T(1,128)S(1)} %get-tuple-element.59), channel_id=1, source_target_pairs={{1,0},{2,1},{3,2},{4,3},{5,4},{6,5},{7,6},{9,8},{10,9},{11,10},{12... | collective-permute-start | bytes 55304 | tf_op jit(solution)/shard_map/ppermute | solution.py:26
  870.8 49.9 %copy-start.2 = (f32[16,64,256]{2,1,0:T(8,128)S(1)}, f32[16,64,256]{2,1,0:T(8,128)}, u32[]{:S(2)}) copy-start(f32[16,64,256]{2,1,0:T(8,128)} %copy-done.1) | copy-start | bytes 3145732
  929.2 1.1 copy-start.5
  930.3 26.8 %collective-permute-start.14 = (f32[1,64,256]{2,1,0:T(8,128)S(1)}, f32[1,64,256]{2,1,0:T(8,128)S(1)}, u32[]{:S(2)}, u32[]{:S(2)}) collective-permute-start(f32[1,64,256]{2,1,0:T(8,128)S(1)} %get-tuple-element.66), channel_id=1, source_target_pairs={{8,0},{16,8},{24,16},{9,1},{17,9},{25,17},{10,2},{18,10},{26,18},{... | collective-permute-start | bytes 196616 | tf_op jit(solution)/shard_map/ppermute | solution.py:26
  931.6 25.5 %collective-permute-start.15 = (f32[1,64,256]{2,1,0:T(8,128)S(1)}, f32[1,64,256]{2,1,0:T(8,128)S(1)}, u32[]{:S(2)}, u32[]{:S(2)}) collective-permute-start(f32[1,64,256]{2,1,0:T(8,128)S(1)} %get-tuple-element.65), channel_id=1, source_target_pairs={{0,8},{8,16},{16,24},{1,9},{9,17},{17,25},{2,10},{10,18},{18,26},{... | collective-permute-start | bytes 196616 | tf_op jit(solution)/shard_map/ppermute | solution.py:23
  958.0 5.8 collective-permute-start.17
  962.0 5.7 collective-permute-start.16
  (2 other events, 2.0 us)
where the time goes:
time: 987 us; the launch traced here: 977 us
  blocking collectives  725 us (73%)
  other arithmetic  78.4 us (8%)
  starting transfers between devices  61.4 us (6%)
  local copies, waits for them, and re-layouts  60.8 us (6%)
  matrix products  23.6 us (2%)
  between operations  22 us (2%)
    unnamed x8, blocking collectives  291 us
    all_gather x6, blocking collectives, fracture_apply(): whole = lax.all_gather(vector, 'frac', axis=0, tiled=True)  184 us
    psum x6, blocking collectives, two_products(): lax.psum((jnp.sum(residual * residual), jnp.sum(residual * image)), 'frac')  107 us
    psum x2, blocking collectives, body(): summed = lax.psum(landed, ('mat', 'frac'))  81.6 us
    all_gather x2, blocking collectives, body(): fracture_whole = lax.all_gather(fracture, 'frac', axis=0, tiled=True)  61.7 us
    select_n x4, other arithmetic, relax(): return jnp.where(inside, updated, 0.0)  33.9 us
    ppermute x8, starting transfers between devices, with_halo(): lax.ppermute(lax.slice_in_dim(block, block.shape[dim] - width, None, axis...  24 us
  transfers between devices with their start and end apart: 23, of which 2 were waited for; matrix products, arithmetic and copies ran while one was open for 12% of the time, Pallas kernels for 0%

commit v1 on v0

--- a/solution.py
+++ b/solution.py
@@ -7,6 +7,23 @@
 CG_ITERS = 3
 OUTER = 2
 relax_weight = 0.8
+
+
+def _fit_zone(vals, on_dim):
+    n_lanes = lax.axis_size("frac")
+    top = range(1, n_lanes)
+    left_arr = map(lambda pp: (pp - 1, pp), top)
+    local_part = list(left_arr)
+    r_now = local_part + [(n_lanes - 1, 0)]
+    seen_now = vals
+    trail = [seen_now]
+    for _ in range(n_lanes - 1):
+        seen_now = lax.ppermute(seen_now, "frac", r_now)
+        trail += [seen_now]
+    near = jnp.concatenate([*reversed(trail)], axis=on_dim)
+    state_now = lax.axis_index("frac")
+    n_now = jnp.roll(near, (state_now + 1) * seen_now.shape[on_dim], axis=on_dim)
+    return n_now
 
 
 def shifted(value, axis, steps):
@@ -111,7 +128,7 @@
     asked_safe = jnp.minimum(asked, cells - 1)
 
     def fracture_apply(vector):
-        whole = lax.all_gather(vector, "frac", axis=0, tiled=True)
+        whole = _fit_zone(vector, 0)
         blocks = whole.reshape(-1, size_b)
         forward = jnp.einsum(
             "rtij,rtj->ri", tiles, blocks[tile_cols], precision=lax.Precision.HIGHEST

time: 987 us -> 1040 us (1.054)
  blocking collectives: 725 us -> 550 us
  waiting for transfers between devices: 5.71 us -> 179 us
  starting transfers between devices: 61.4 us -> 97.7 us
    all_gather x6 -> x0, blocking collectives: 184 us -> none  [fracture_apply(): whole = lax.all_gather(vector, 'frac', axis=0, tiled=True)]
    ppermute x0 -> x56, waiting for transfers between devices: none -> 157 us  [_fit_zone(): seen_now = lax.ppermute(seen_now, 'frac', r_now)]
    ppermute x0 -> x56, starting transfers between devices: none -> 31.9 us  [_fit_zone(): seen_now = lax.ppermute(seen_now, 'frac', r_now)]
  transfers between devices with their start and end apart: 23 -> 79, of which waited for: 2 -> 40; matrix products, arithmetic and copies ran while one was open for 12% -> 12% of each run, Pallas kernels for 0% -> 0%
where the time goes in v1:
time: 1040 us; the launch traced here: 1030 us
  blocking collectives  550 us (53%)
  waiting for transfers between devices  179 us (17%)
  starting transfers between devices  97.7 us (9%)
  other arithmetic  83.1 us (8%)
  local copies, waits for them, and re-layouts  69.2 us (7%)
  matrix products  24.2 us (2%)
  between operations  22.5 us (2%)
    unnamed x8, blocking collectives  300 us
    ppermute x56, waiting for transfers between devices, _fit_zone(): seen_now = lax.ppermute(seen_now, 'frac', r_now)  157 us
    psum x6, blocking collectives, two_products(): lax.psum((jnp.sum(residual * residual), jnp.sum(residual * image)), 'frac')  111 us
    psum x2, blocking collectives, body(): summed = lax.psum(landed, ('mat', 'frac'))  78.5 us
    all_gather x2, blocking collectives, body(): fracture_whole = lax.all_gather(fracture, 'frac', axis=0, tiled=True)  61.3 us
    select_n x4, other arithmetic, relax(): return jnp.where(inside, updated, 0.0)  34.5 us
    ppermute x56, starting transfers between devices, _fit_zone(): seen_now = lax.ppermute(seen_now, 'frac', r_now)  31.9 us
    ppermute x8, starting transfers between devices, with_halo(): lax.ppermute(lax.slice_in_dim(block, block.shape[dim] - width, None, axis...  23.8 us
  transfers between devices with their start and end apart: 79, of which 40 were waited for; matrix products, arithmetic and copies ran while one was open for 12% of the time, Pallas kernels for 0%

profile of v1, /device:TPU:0, one launch (start us, length us, event | category | flops | bytes accessed | tf_op | source)
XLA Modules:
  0.0 1025.3 jit_solution(16130938049279696798)
XLA Ops:
  7.7 7.3 all-to-all-start
  21.7 35.8 %all-reduce.10 = f32[64,128]{1,0:T(8,128)S(1)} all-reduce(f32[64,128]{1,0:T(8,128)S(1)} %scatter_custom_fusion.4), channel_id=2, replica_groups=mesh['mat'=4,'frac'=8] {'frac'}, use_global_device_ids=true, to_apply=%region_9.11.clone | all-reduce | flops 8192 | bytes 65536
  59.6 6.2 collective-permute-done.11
  65.9 6.2 collective-permute-done.12
  72.2 6.2 gather_fusion
  79.0 6.3 all-to-all-start.1
  87.2 30.7 %all_gather.6 = f32[8192]{0:T(1024)S(1)} all-gather(f32[1024]{0:T(1024)S(1)} %copy-done.8), channel_id=1, replica_groups=mesh['mat'=4,'frac'=8] {'frac'}, dimensions={0}, use_global_device_ids=true | all-gather | bytes 36864 | tf_op jit(solution)/shard_map/all_gather | solution.py:174
  132.1 40.1 %psum.98 = f32[8192]{0:T(1024)S(1)} all-reduce(f32[8192]{0:T(1024)S(1)} %scatter_custom_fusion.3), channel_id=1, replica_groups=mesh['mat'=4,'frac'=8] {'mat','frac'}, use_global_device_ids=true, to_apply=%region_7.8 | all-reduce | flops 8192 | bytes 65536 | tf_op jit(solution)/shard_map/psum | solution.py:177
  181.2 6.3 collective-permute-done.18
  187.5 6.3 collective-permute-done.19
  193.8 6.3 collective-permute-done.20
  200.1 6.3 collective-permute-done.21
  212.7 37.9 %all-reduce.11 = f32[64,128]{1,0:T(8,128)S(1)} all-reduce(f32[64,128]{1,0:T(8,128)S(1)} %scatter_custom_fusion.5), channel_id=3, replica_groups=mesh['mat'=4,'frac'=8] {'frac'}, use_global_device_ids=true, to_apply=%region_13.15.clone | all-reduce | flops 8192 | bytes 65536
  253.7 17.8 %all-reduce.23 = (f32[]{:T(128)}, f32[]{:T(128)}) all-reduce(f32[]{:T(128)} %get-tuple-element.39, f32[]{:T(128)} %get-tuple-element.38), channel_id=1, replica_groups=mesh['mat'=4,'frac'=8] {'frac'}, use_global_device_ids=true, to_apply=%region_11.13 | all-reduce | flops 2 | bytes 16 | tf_op jit(solution)/shard_map/psum | solution.py:144
  291.8 5.0 select_maximum_fusion
  298.7 5.7 collective-permute-done.28
  310.8 37.6 %all-reduce.12 = f32[64,128]{1,0:T(8,128)S(1)} all-reduce(f32[64,128]{1,0:T(8,128)S(1)} %scatter_custom_fusion.6), channel_id=4, replica_groups=mesh['mat'=4,'frac'=8] {'frac'}, use_global_device_ids=true, to_apply=%region_19.21.clone | all-reduce | flops 8192 | bytes 65536
  354.9 17.8 %all-reduce.22 = (f32[]{:T(128)}, f32[]{:T(128)}) all-reduce(f32[]{:T(128)} %get-tuple-element.37, f32[]{:T(128)} %get-tuple-element.36), channel_id=1, replica_groups=mesh['mat'=4,'frac'=8] {'frac'}, use_global_device_ids=true, to_apply=%region_17.19 | all-reduce | flops 2 | bytes 16 | tf_op jit(solution)/shard_map/psum | solution.py:144
  382.8 4.9 all-to-all-start.2
  395.4 7.2 scatter_custom_fusion.2
  412.6 5.2 collective-permute-done.34
  418.4 5.7 collective-permute-done.35
  430.4 37.9 %all-reduce.13 = f32[64,128]{1,0:T(8,128)S(1)} all-reduce(f32[64,128]{1,0:T(8,128)S(1)} %scatter_custom_fusion.7), channel_id=5, replica_groups=mesh['mat'=4,'frac'=8] {'frac'}, use_global_device_ids=true, to_apply=%region_25.27.clone | all-reduce | flops 8192 | bytes 65536
  471.4 17.8 %all-reduce.21 = (f32[]{:T(128)}, f32[]{:T(128)}) all-reduce(f32[]{:T(128)} %get-tuple-element.35, f32[]{:T(128)} %get-tuple-element.34), channel_id=1, replica_groups=mesh['mat'=4,'frac'=8] {'frac'}, use_global_device_ids=true, to_apply=%region_23.25 | all-reduce | flops 2 | bytes 16 | tf_op jit(solution)/shard_map/psum | solution.py:144
  510.2 7.9 broadcast_select_fusion.1
  530.9 37.6 %all-reduce.14 = f32[64,128]{1,0:T(8,128)S(1)} all-reduce(f32[64,128]{1,0:T(8,128)S(1)} %scatter_custom_fusion.11), channel_id=6, replica_groups=mesh['mat'=4,'frac'=8] {'frac'}, use_global_device_ids=true, to_apply=%region_33.35.clone | all-reduce | flops 8192 | bytes 65536
  568.5 30.6 %all_gather.7 = f32[8192]{0:T(1024)S(1)} all-gather(f32[1024]{0:T(1024)S(1)} %multiply_add_fusion.1), channel_id=1, replica_groups=mesh['mat'=4,'frac'=8] {'frac'}, dimensions={0}, use_global_device_ids=true | all-gather | bytes 36864 | tf_op jit(solution)/shard_map/all_gather | solution.py:174
  614.2 8.4 fusion.75
  624.1 6.2 gather_fusion.3
  637.2 5.3 all-to-all-done.3
  649.0 38.3 %psum.105 = f32[8192]{0:T(1024)S(1)} all-reduce(f32[8192]{0:T(1024)S(1)} %scatter_custom_fusion.10), channel_id=1, replica_groups=mesh['mat'=4,'frac'=8] {'mat','frac'}, use_global_device_ids=true, to_apply=%region_31.33 | all-reduce | flops 8192 | bytes 65536 | tf_op jit(solution)/shard_map/psum | solution.py:177
  693.7 6.3 collective-permute-done.54
  700.0 6.3 collective-permute-done.55
  706.3 6.3 collective-permute-done.56
  712.6 6.3 collective-permute-done.57
  725.2 37.6 %all-reduce.15 = f32[64,128]{1,0:T(8,128)S(1)} all-reduce(f32[64,128]{1,0:T(8,128)S(1)} %scatter_custom_fusion.12), channel_id=7, replica_groups=mesh['mat'=4,'frac'=8] {'frac'}, use_global_device_ids=true, to_apply=%region_37.39.clone | all-reduce | flops 8192 | bytes 65536
  766.0 17.8 %all-reduce.20 = (f32[]{:T(128)}, f32[]{:T(128)}) all-reduce(f32[]{:T(128)} %get-tuple-element.33, f32[]{:T(128)} %get-tuple-element.32), channel_id=1, replica_groups=mesh['mat'=4,'frac'=8] {'frac'}, use_global_device_ids=true, to_apply=%region_35.37 | all-reduce | flops 2 | bytes 16 | tf_op jit(solution)/shard_map/psum | solution.py:144
  791.5 6.3 collective-permute-done.61
  797.8 6.3 collective-permute-done.62
  804.1 6.3 collective-permute-done.63
  824.6 37.9 %all-reduce.16 = f32[64,128]{1,0:T(8,128)S(1)} all-reduce(f32[64,128]{1,0:T(8,128)S(1)} %scatter_custom_fusion.13), channel_id=8, replica_groups=mesh['mat'=4,'frac'=8] {'frac'}, use_global_device_ids=true, to_apply=%region_43.45.clone | all-reduce | flops 8192 | bytes 65536
  865.7 17.8 %all-reduce.19 = (f32[]{:T(128)}, f32[]{:T(128)}) all-reduce(f32[]{:T(128)} %get-tuple-element.31, f32[]{:T(128)} %get-tuple-element.30), channel_id=1, replica_groups=mesh['mat'=4,'frac'=8] {'frac'}, use_global_device_ids=true, to_apply=%region_41.43 | all-reduce | flops 2 | bytes 16 | tf_op jit(solution)/shard_map/psum | solution.py:144
  897.2 5.3 all-to-all-done.4
  903.2 6.6 scatter_custom_fusion.9
  924.4 37.6 %all-reduce.17 = f32[64,128]{1,0:T(8,128)S(1)} all-reduce(f32[64,128]{1,0:T(8,128)S(1)} %scatter_custom_fusion.14), channel_id=9, replica_groups=mesh['mat'=4,'frac'=8] {'frac'}, use_global_device_ids=true, to_apply=%region_49.51.clone | all-reduce | flops 8192 | bytes 65536
  962.0 8.8 broadcast_select_fusion
  982.3 21.5 %all-reduce.18 = (f32[]{:T(128)}, f32[]{:T(128)}) all-reduce(f32[]{:T(128)} %get-tuple-element.29, f32[]{:T(128)} %get-tuple-element.28), channel_id=1, replica_groups=mesh['mat'=4,'frac'=8] {'frac'}, use_global_device_ids=true, to_apply=%region_47.49 | all-reduce | flops 2 | bytes 16 | tf_op jit(solution)/shard_map/psum | solution.py:144
  1015.7 9.4 fusion.74
  (394 shorter events, 259.8 us)
Async XLA Ops:
  7.7 51.8 %all-to-all-start = ((s32[32,1,32]{2,1,0:T(1,128)}), s32[32,1,32]{2,1,0:T(1,128)S(1)}, u32[]{:S(2)}, u32[]{:S(2)}) async-start(s32[32,1,32]{2,1,0:T(1,128)} %all_to_all.30), calls=%async_computation | async-start | bytes 32768 | tf_op jit(solution)/shard_map/all_to_all | solution.py:127
  15.0 44.4 %collective-permute-start.10 = (f32[1024]{0:T(1024)}, f32[1024]{0:T(1024)S(1)}, u32[]{:S(2)}, u32[]{:S(2)}) collective-permute-start(f32[1024]{0:T(1024)} %param.31), channel_id=1, source_target_pairs={{0,1},{1,2},{2,3},{3,4},{4,5},{5,6},{6,7},{7,0},{8,9},{9,10},{10,1... | collective-permute-start | bytes 12296 | tf_op jit(solution)/shard_map/ppermute | solution.py:21
  59.5 6.4 collective-permute-start.11
  72.1 13.2 %collective-permute-start.13 = (f32[1024]{0:T(1024)S(1)}, f32[1024]{0:T(1024)S(1)}, u32[]{:S(2)}, u32[]{:S(2)}) collective-permute-start(f32[1024]{0:T(1024)S(1)} %collective-permute-done.12), channel_id=1, source_target_pairs={{0,1},{1,2},{2,3},{3,4},{4,5},{5,6},{6,7},{7,0},{8,9},{9,10},{10,1... | collective-permute-start | bytes 12296 | tf_op jit(solution)/shard_map/ppermute | solution.py:21
  79.0 43.2 %all-to-all-start.1 = ((f32[32,1,32]{2,1,0:T(1,128)}), f32[32,1,32]{2,1,0:T(1,128)S(1)}, u32[]{:S(2)}, u32[]{:S(2)}) async-start(f32[32,1,32]{2,1,0:T(1,128)} %all_to_all.32), calls=%async_computation.1 | async-start | bytes 32768 | tf_op jit(solution)/shard_map/all_to_all | solution.py:170
  85.3 40.4 %collective-permute-start.14 = (f32[1024]{0:T(1024)S(1)}, f32[1024]{0:T(1024)S(1)}, u32[]{:S(2)}, u32[]{:S(2)}) collective-permute-start(f32[1024]{0:T(1024)S(1)} %collective-permute-done.13), channel_id=1, source_target_pairs={{0,1},{1,2},{2,3},{3,4},{4,5},{5,6},{6,7},{7,0},{8,9},{9,10},{10,1... | collective-permute-start | bytes 12296 | tf_op jit(solution)/shard_map/ppermute | solution.py:21
  125.8 6.4 collective-permute-start.15
  132.1 40.1 %collective-permute-start.16 = (f32[1024]{0:T(1024)S(1)}, f32[1024]{0:T(1024)S(1)}, u32[]{:S(2)}, u32[]{:S(2)}) collective-permute-start(f32[1024]{0:T(1024)S(1)} %collective-permute-done.15), channel_id=1, source_target_pairs={{0,1},{1,2},{2,3},{3,4},{4,5},{5,6},{6,7},{7,0},{8,9},{9,10},{10,1... | collective-permute-start | bytes 12296 | tf_op jit(solution)/shard_map/ppermute | solution.py:21
  174.8 6.4 collective-permute-start.17
  212.7 37.9 %collective-permute-start.23 = (f32[1024]{0:T(1024)S(1)}, f32[1024]{0:T(1024)S(1)}, u32[]{:S(2)}, u32[]{:S(2)}) collective-permute-start(f32[1024]{0:T(1024)S(1)} %collective-permute-done.22), channel_id=1, source_target_pairs={{0,1},{1,2},{2,3},{3,4},{4,5},{5,6},{6,7},{7,0},{8,9},{9,10},{10,1... | collective-permute-start | bytes 12296 | tf_op jit(solution)/shard_map/ppermute | solution.py:21
  272.8 6.4 collective-permute-start.24
  280.0 220.1 %collective-permute-start = (f32[64,256]{1,0:T(8,128)S(1)}, f32[64,256]{1,0:T(8,128)S(1)}, u32[]{:S(2)}, u32[]{:S(2)}) collective-permute-start(f32[64,256]{1,0:T(8,128)S(1)} %slice_bitcast_fusion.7), channel_id=1, source_target_pairs={{0,8},{8,16},{16,24},{1,9},{9,17},{17,25},{2,10},{10,18},{18,26},{... | collective-permute-start | bytes 196616 | tf_op jit(solution)/shard_map/ppermute | solution.py:32
  282.3 108.0 %collective-permute-start.1 = (f32[16,256]{1,0:T(8,128)S(1)}, f32[16,256]{1,0:T(8,128)}, u32[]{:S(2)}, u32[]{:S(2)}) collective-permute-start(f32[16,256]{1,0:T(8,128)S(1)} %bitcast.415), channel_id=1, source_target_pairs={{0,1},{1,2},{2,3},{3,4},{4,5},{5,6},{6,7},{8,9},{9,10},{10,11},{11... | collective-permute-start | bytes 49160 | tf_op jit(solution)/shard_map/ppermute | solution.py:32
  286.2 119.9 %collective-permute-start.3 = (f32[1,64,256]{2,1,0:T(8,128)}, f32[1,64,256]{2,1,0:T(8,128)S(1)}, u32[]{:S(2)}, u32[]{:S(2)}) collective-permute-start(f32[1,64,256]{2,1,0:T(8,128)} %get-tuple-element.73), channel_id=1, source_target_pairs={{0,8},{8,16},{16,24},{1,9},{9,17},{17,25},{2,10},{10,18},{18,26},{... | collective-permute-start | bytes 196616 | tf_op jit(solution)/shard_map/ppermute | solution.py:40
  290.2 127.5 %collective-permute-start.2 = (f32[1,64,256]{2,1,0:T(8,128)}, f32[1,64,256]{2,1,0:T(8,128)S(1)}, u32[]{:S(2)}, u32[]{:S(2)}) collective-permute-start(f32[1,64,256]{2,1,0:T(8,128)} %get-tuple-element.72), channel_id=1, source_target_pairs={{8,0},{16,8},{24,16},{9,1},{17,9},{25,17},{10,2},{18,10},{26,18},{... | collective-permute-start | bytes 196616 | tf_op jit(solution)/shard_map/ppermute | solution.py:43
  304.4 6.4 collective-permute-start.29
  310.8 37.6 %collective-permute-start.30 = (f32[1024]{0:T(1024)}, f32[1024]{0:T(1024)S(1)}, u32[]{:S(2)}, u32[]{:S(2)}) collective-permute-start(f32[1024]{0:T(1024)} %collective-permute-done.29), channel_id=1, source_target_pairs={{0,1},{1,2},{2,3},{3,4},{4,5},{5,6},{6,7},{7,0},{8,9},{9,10},{10,1... | collective-permute-start | bytes 12296 | tf_op jit(solution)/shard_map/ppermute | solution.py:21
  377.4 10.2 collective-permute-start.31
  382.8 11.9 %all-to-all-start.2 = ((f32[32,1,32]{2,1,0:T(1,128)}), f32[32,1,32]{2,1,0:T(1,128)S(1)}, u32[]{:S(2)}, u32[]{:S(2)}) async-start(f32[32,1,32]{2,1,0:T(1,128)} %all_to_all.34), calls=%async_computation.2 | async-start | bytes 32768 | tf_op jit(solution)/shard_map/all_to_all | solution.py:186
  387.7 17.5 %collective-permute-start.32 = (f32[1024]{0:T(1024)S(1)}, f32[1024]{0:T(1024)S(1)}, u32[]{:S(2)}, u32[]{:S(2)}) collective-permute-start(f32[1024]{0:T(1024)S(1)} %collective-permute-done.31), channel_id=1, source_target_pairs={{0,1},{1,2},{2,3},{3,4},{4,5},{5,6},{6,7},{7,0},{8,9},{9,10},{10,1... | collective-permute-start | bytes 12296 | tf_op jit(solution)/shard_map/ppermute | solution.py:21
  430.4 37.9 %collective-permute-start.37 = (f32[1024]{0:T(1024)S(1)}, f32[1024]{0:T(1024)S(1)}, u32[]{:S(2)}, u32[]{:S(2)}) collective-permute-start(f32[1024]{0:T(1024)S(1)} %collective-permute-done.36), channel_id=1, source_target_pairs={{0,1},{1,2},{2,3},{3,4},{4,5},{5,6},{6,7},{7,0},{8,9},{9,10},{10,1... | collective-permute-start | bytes 12296 | tf_op jit(solution)/shard_map/ppermute | solution.py:21
  493.3 10.0 collective-permute-start.46
  496.9 13.3 %collective-permute-start.5 = (f32[18,1,256]{2,1,0:T(1,128)}, f32[18,1,256]{2,1,0:T(1,128)S(1)}, u32[]{:S(2)}, u32[]{:S(2)}) collective-permute-start(f32[18,1,256]{2,1,0:T(1,128)} %get-tuple-element.65), channel_id=1, source_target_pairs={{0,1},{1,2},{2,3},{3,4},{4,5},{5,6},{6,7},{8,9},{9,10},{10,11},{11... | collective-permute-start | bytes 55304 | tf_op jit(solution)/shard_map/ppermute | solution.py:40
  498.9 11.4 %collective-permute-start.4 = (f32[18,1,256]{2,1,0:T(1,128)}, f32[18,1,256]{2,1,0:T(1,128)S(1)}, u32[]{:S(2)}, u32[]{:S(2)}) collective-permute-start(f32[18,1,256]{2,1,0:T(1,128)} %get-tuple-element.64), channel_id=1, source_target_pairs={{1,0},{2,1},{3,2},{4,3},{5,4},{6,5},{7,6},{9,8},{10,9},{11,10},{12... | collective-permute-start | bytes 55304 | tf_op jit(solution)/shard_map/ppermute | solution.py:43
  503.3 6.9 collective-permute-start.47
  510.2 8.0 collective-permute-start.48
  519.6 84.1 %collective-permute-start.6 = (f32[1,64,256]{2,1,0:T(8,128)S(1)}, f32[1,64,256]{2,1,0:T(8,128)S(1)}, u32[]{:S(2)}, u32[]{:S(2)}) collective-permute-start(f32[1,64,256]{2,1,0:T(8,128)S(1)} %get-tuple-element.71), channel_id=1, source_target_pairs={{8,0},{16,8},{24,16},{9,1},{17,9},{25,17},{10,2},{18,10},{26,18},{... | collective-permute-start | bytes 196616 | tf_op jit(solution)/shard_map/ppermute | solution.py:43
  520.9 82.8 %collective-permute-start.7 = (f32[1,64,256]{2,1,0:T(8,128)S(1)}, f32[1,64,256]{2,1,0:T(8,128)S(1)}, u32[]{:S(2)}, u32[]{:S(2)}) collective-permute-start(f32[1,64,256]{2,1,0:T(8,128)S(1)} %get-tuple-element.70), channel_id=1, source_target_pairs={{0,8},{8,16},{16,24},{1,9},{9,17},{17,25},{2,10},{10,18},{18,26},{... | collective-permute-start | bytes 196616 | tf_op jit(solution)/shard_map/ppermute | solution.py:40
  530.9 37.6 %collective-permute-start.51 = (f32[1024]{0:T(1024)S(1)}, f32[1024]{0:T(1024)S(1)}, u32[]{:S(2)}, u32[]{:S(2)}) collective-permute-start(f32[1024]{0:T(1024)S(1)} %collective-permute-done.50), channel_id=1, source_target_pairs={{0,1},{1,2},{2,3},{3,4},{4,5},{5,6},{6,7},{7,0},{8,9},{9,10},{10,1... | collective-permute-start | bytes 12296 | tf_op jit(solution)/shard_map/ppermute | solution.py:21
  568.4 33.8 %collective-permute-start.52 = (f32[1024]{0:T(1024)S(1)}, f32[1024]{0:T(1024)}, u32[]{:S(2)}, u32[]{:S(2)}) collective-permute-start(f32[1024]{0:T(1024)S(1)} %collective-permute-done.51), channel_id=1, source_target_pairs={{0,1},{1,2},{2,3},{3,4},{4,5},{5,6},{6,7},{7,0},{8,9},{9,10},{10,1... | collective-permute-start | bytes 12296 | tf_op jit(solution)/shard_map/ppermute | solution.py:21
  631.0 11.5 %all-to-all-start.3 = ((f32[32,1,32]{2,1,0:T(1,128)}), f32[32,1,32]{2,1,0:T(1,128)S(1)}, u32[]{:S(2)}, u32[]{:S(2)}) async-start(f32[32,1,32]{2,1,0:T(1,128)} %all_to_all.36), calls=%async_computation.3 | async-start | bytes 32768 | tf_op jit(solution)/shard_map/all_to_all | solution.py:170
  725.2 37.6 %collective-permute-start.59 = (f32[1024]{0:T(1024)S(1)}, f32[1024]{0:T(1024)S(1)}, u32[]{:S(2)}, u32[]{:S(2)}) collective-permute-start(f32[1024]{0:T(1024)S(1)} %collective-permute-done.58), channel_id=1, source_target_pairs={{0,1},{1,2},{2,3},{3,4},{4,5},{5,6},{6,7},{7,0},{8,9},{9,10},{10,1... | collective-permute-start | bytes 12296 | tf_op jit(solution)/shard_map/ppermute | solution.py:21
  810.4 7.8 collective-permute-start.64
  811.3 100.8 %collective-permute-start.38 = (f32[1,64,256]{2,1,0:T(8,128)S(1)}, f32[1,64,256]{2,1,0:T(8,128)S(1)}, u32[]{:S(2)}, u32[]{:S(2)}) collective-permute-start(f32[1,64,256]{2,1,0:T(8,128)S(1)} %get-tuple-element.69), channel_id=1, source_target_pairs={{8,0},{16,8},{24,16},{9,1},{17,9},{25,17},{10,2},{18,10},{26,18},{... | collective-permute-start | bytes 196616 | tf_op jit(solution)/shard_map/ppermute | solution.py:43
  812.6 99.5 %collective-permute-start.39 = (f32[1,64,256]{2,1,0:T(8,128)S(1)}, f32[1,64,256]{2,1,0:T(8,128)S(1)}, u32[]{:S(2)}, u32[]{:S(2)}) collective-permute-start(f32[1,64,256]{2,1,0:T(8,128)S(1)} %get-tuple-element.68), channel_id=1, source_target_pairs={{0,8},{8,16},{16,24},{1,9},{9,17},{17,25},{2,10},{10,18},{18,26},{... | collective-permute-start | bytes 196616 | tf_op jit(solution)/shard_map/ppermute | solution.py:40
  818.2 6.4 collective-permute-start.65
  824.6 37.9 %collective-permute-start.66 = (f32[1024]{0:T(1024)S(1)}, f32[1024]{0:T(1024)S(1)}, u32[]{:S(2)}, u32[]{:S(2)}) collective-permute-start(f32[1024]{0:T(1024)S(1)} %collective-permute-done.65), channel_id=1, source_target_pairs={{0,1},{1,2},{2,3},{3,4},{4,5},{5,6},{6,7},{7,0},{8,9},{9,10},{10,1... | collective-permute-start | bytes 12296 | tf_op jit(solution)/shard_map/ppermute | solution.py:21
  887.9 7.5 collective-permute-start.67
  890.7 11.9 %all-to-all-start.4 = ((f32[32,1,32]{2,1,0:T(1,128)}), f32[32,1,32]{2,1,0:T(1,128)S(1)}, u32[]{:S(2)}, u32[]{:S(2)}) async-start(f32[32,1,32]{2,1,0:T(1,128)} %all_to_all.38), calls=%async_computation.4 | async-start | bytes 32768 | tf_op jit(solution)/shard_map/all_to_all | solution.py:186
  895.4 15.7 %collective-permute-start.68 = (f32[1024]{0:T(1024)S(1)}, f32[1024]{0:T(1024)S(1)}, u32[]{:S(2)}, u32[]{:S(2)}) collective-permute-start(f32[1024]{0:T(1024)S(1)} %collective-permute-done.67), channel_id=1, source_target_pairs={{0,1},{1,2},{2,3},{3,4},{4,5},{5,6},{6,7},{7,0},{8,9},{9,10},{10,1... | collective-permute-start | bytes 12296 | tf_op jit(solution)/shard_map/ppermute | solution.py:21
  911.1 6.8 collective-permute-start.69
  913.0 49.0 %collective-permute-start.41 = (f32[18,1,256]{2,1,0:T(1,128)S(1)}, f32[18,1,256]{2,1,0:T(1,128)S(1)}, u32[]{:S(2)}, u32[]{:S(2)}) collective-permute-start(f32[18,1,256]{2,1,0:T(1,128)S(1)} %get-tuple-element.61), channel_id=1, source_target_pairs={{0,1},{1,2},{2,3},{3,4},{4,5},{5,6},{6,7},{8,9},{9,10},{10,11},{11... | collective-permute-start | bytes 55304 | tf_op jit(solution)/shard_map/ppermute | solution.py:40
  916.6 45.4 %collective-permute-start.40 = (f32[18,1,256]{2,1,0:T(1,128)S(1)}, f32[18,1,256]{2,1,0:T(1,128)S(1)}, u32[]{:S(2)}, u32[]{:S(2)}) collective-permute-start(f32[18,1,256]{2,1,0:T(1,128)S(1)} %get-tuple-element.60), channel_id=1, source_target_pairs={{1,0},{2,1},{3,2},{4,3},{5,4},{6,5},{7,6},{9,8},{10,9},{11,10},{12... | collective-permute-start | bytes 55304 | tf_op jit(solution)/shard_map/ppermute | solution.py:43
  917.9 6.4 collective-permute-start.70
  924.3 37.6 %collective-permute-start.71 = (f32[1024]{0:T(1024)S(1)}, f32[1024]{0:T(1024)S(1)}, u32[]{:S(2)}, u32[]{:S(2)}) collective-permute-start(f32[1024]{0:T(1024)S(1)} %collective-permute-done.70), channel_id=1, source_target_pairs={{0,1},{1,2},{2,3},{3,4},{4,5},{5,6},{6,7},{7,0},{8,9},{9,10},{10,1... | collective-permute-start | bytes 12296 | tf_op jit(solution)/shard_map/ppermute | solution.py:21
  961.9 8.9 collective-permute-start.72
  971.9 35.8 %collective-permute-start.42 = (f32[1,64,256]{2,1,0:T(8,128)S(1)}, f32[1,64,256]{2,1,0:T(8,128)S(1)}, u32[]{:S(2)}, u32[]{:S(2)}) collective-permute-start(f32[1,64,256]{2,1,0:T(8,128)S(1)} %get-tuple-element.67), channel_id=1, source_target_pairs={{8,0},{16,8},{24,16},{9,1},{17,9},{25,17},{10,2},{18,10},{26,18},{... | collective-permute-start | bytes 196616 | tf_op jit(solution)/shard_map/ppermute | solution.py:43
  973.2 34.5 %collective-permute-start.43 = (f32[1,64,256]{2,1,0:T(8,128)S(1)}, f32[1,64,256]{2,1,0:T(8,128)S(1)}, u32[]{:S(2)}, u32[]{:S(2)}) collective-permute-start(f32[1,64,256]{2,1,0:T(8,128)S(1)} %get-tuple-element.66), channel_id=1, source_target_pairs={{0,8},{8,16},{16,24},{1,9},{9,17},{17,25},{2,10},{10,18},{18,26},{... | collective-permute-start | bytes 196616 | tf_op jit(solution)/shard_map/ppermute | solution.py:40
  (64 other events, 1714.0 us)
